TPU v7x, 64 devices: a 2x2x8 block of a 4x4x8 slice. The times are simulated.
64 devices in a mesh: rep: 4 (over x, y), dp: 16 (over z, core).
Axes of the slice: x: 2, y: 2, z: 8, core: 2. Of those that a mesh axis runs over, the one named last changes fastest.
The devices are a block of a 4x4x8 slice.
Arguments:
- x: bfloat16 [64, 2048, 896], P(('rep', 'dp')), parts along dimension 0
- dy: bfloat16 [64, 2048, 896], P(('rep', 'dp')), parts along dimension 0
- w_gate: bfloat16 [2, 896, 2304], replicated
- w_up: bfloat16 [2, 896, 2304], replicated
- w_down: bfloat16 [2, 2304, 896], replicated
- m_w_gate: float32 [2, 896, 2304], P(None, 'dp')
- m_w_up: float32 [2, 896, 2304], P(None, 'dp')
- m_w_down: float32 [2, 2304, 896], P(None, 'dp')
- v_w_gate: float32 [2, 896, 2304], P(None, 'dp')
- v_w_up: float32 [2, 896, 2304], P(None, 'dp')
- v_w_down: float32 [2, 2304, 896], P(None, 'dp')
Outputs:
- output 1: bfloat16 [8, 896, 2304], P('rep'), parts along dimension 0
- output 2: bfloat16 [8, 896, 2304], P('rep'), parts along dimension 0
- output 3: bfloat16 [8, 2304, 896], P('rep'), parts along dimension 0
- output 4: float32 [8, 896, 2304], P('rep', 'dp'), parts along dimension 0
- output 5: float32 [8, 896, 2304], P('rep', 'dp'), parts along dimension 0
- output 6: float32 [8, 2304, 896], P('rep', 'dp'), parts along dimension 0
- output 7: float32 [8, 896, 2304], P('rep', 'dp'), parts along dimension 0
- output 8: float32 [8, 896, 2304], P('rep', 'dp'), parts along dimension 0
- output 9: float32 [8, 2304, 896], P('rep', 'dp'), parts along dimension 0
There are 4 independent parts. A program takes and returns all parts, laid end to end along the dimension named above; an argument that names none is the same for every part.
All inputs are finite; a program needn't handle non-finite values.
Results may differ from a plain program's by a relative error of at most 0.022.
Values are sent between devices in bfloat16 or wider.
A program may use at most 768 MiB of HBM per device.

v0:
```python
import jax
import jax.numpy as jnp
from jax import lax

NAMES = ("w_gate", "w_up", "w_down")


def matmul(a, w):
    return jnp.dot(a, w, preferred_element_type=jnp.float32).astype(jnp.bfloat16)


def normed(h):
    wide = h.astype(jnp.float32)
    scale = lax.rsqrt(jnp.mean(wide**2, -1, keepdims=True) + 1e-6)
    return (wide * scale).astype(jnp.bfloat16)


def layer(h, w):
    a = normed(h)
    gate = jnp.dot(a, w["w_gate"], preferred_element_type=jnp.float32)
    up = jnp.dot(a, w["w_up"], preferred_element_type=jnp.float32)
    return h + matmul((jax.nn.silu(gate) * up).astype(jnp.bfloat16), w["w_down"])


def adamw(w, m, v, g):
    m = 0.9 * m + 0.1 * g
    v = 0.95 * v + 0.05 * g * g
    step = m * lax.rsqrt(v + 1e-8) + 0.1 * w
    return (w - 0.02 * step).astype(jnp.bfloat16), m, v


def clipped(gradients, sum_of_squares, count):
    factor = jnp.minimum(1.0, 0.5 * lax.rsqrt(sum_of_squares / count + 1e-30))
    return [g * factor for g in gradients]


def stack(weights, h):
    for number in range(weights["w_gate"].shape[0]):
        h = layer(h, {name: w[number] for name, w in weights.items()})
    return h


def solution(mesh):
    groups = mesh.shape["rep"]

    def step(x, dy, *arrays):
        weights, m, v = (arrays[i : i + 3] for i in (0, 3, 6))
        x, dy = (t.reshape(groups, -1, *t.shape[1:]) for t in (x, dy))

        def of_a_group(x, dy):
            _, back = jax.vjp(lambda w: stack(w, x), dict(zip(NAMES, weights, strict=True)))
            by_weights = back(dy)[0]
            gradients = [by_weights[name].astype(jnp.float32) for name in NAMES]
            gradients = clipped(gradients, sum(jnp.sum(g * g) for g in gradients), sum(g.size for g in gradients))
            new = [adamw(w.astype(jnp.float32), m, v, g) for w, m, v, g in zip(weights, m, v, gradients, strict=True)]
            return tuple(one[which] for which in range(3) for one in new)

        return tuple(t.reshape(-1, *t.shape[2:]) for t in jax.vmap(of_a_group)(x, dy))

    return step
```

profile of v0, /device:TPU:21, one launch (start us, length us, event | category | flops | bytes accessed | tf_op | source)
XLA Modules:
  0.0 1066.6 jit_solution(10373374576408244320)
XLA Ops:
  21.4 15.5 %fusion.182 = f32[2048,2304]{1,0:T(8,128)} fusion(bf16[2,896,2304]{2,1,0:T(8,128)(2,1)} %param.12, bf16[1,2048,896]{2,1,0:T(8,128)(2,1)S(1)} %copy-done.17, f32[2048]{0:T(1024)S(1)} %add_rsqrt_fusion), kind=kOutput, calls=%fused_computation.230 | convolution fusion | flops 8461221888 | bytes 26681344 | tf_op jit(solution)/vmap(jvp())/dot_general | solution.py:20
  36.9 21.3 %fusion.156 = (bf16[1,1,2048,2304]{3,2,1,0:T(8,128)(2,1)}, f32[2048,2304]{1,0:T(8,128)}) fusion(f32[2048,2304]{1,0:T(8,128)} %fusion.182, bf16[2,896,2304]{2,1,0:T(8,128)(2,1)} %param.15, bf16[1,2048,896]{2,1,0:T(8,128)(2,1)} %param.14, f32[2048]{0:T(1024)S(1)} %add_rsqrt_fusion), kind=kOutput, calls=%fused_computation.191 | convolution fusion | flops 8489533440 | bytes 54992896 | tf_op jit(solution)/vmap(jvp())/dot_general | solution.py:21
  58.2 13.8 %fusion.168 = (f32[2048]{0:T(1024)S(1)}, bf16[1,1,2048,896]{2,3,1,0:T(8,128)(2,1)S(1)}) fusion(bf16[2,2304,896]{2,1,0:T(8,128)(2,1)} %param.16, bf16[1,1,2048,2304]{3,2,1,0:T(8,128)(2,1)} %get-tuple-element.263, bf16[1,2048,896]{1,2,0:T(8,128)(2,1)} %copy), kind=kOutput, calls=%fused_computation.215 | convolution fusion | flops 8464889856 | bytes 20914176 | tf_op jit(solution)/vmap(jvp())/dot_general | solution.py:9
  76.8 15.1 %fusion.172 = f32[2048,2304]{1,0:T(8,128)} fusion(bf16[1,1,2048,896]{2,3,1,0:T(8,128)(2,1)S(1)} %fusion.169, bf16[2,896,2304]{2,1,0:T(8,128)(2,1)} %param.12), kind=kOutput, calls=%fused_computation.220 | convolution fusion | flops 8455716864 | bytes 26673152 | tf_op jit(solution)/vmap(jvp())/dot_general | solution.py:20
  91.9 23.4 %fusion.155 = (bf16[1,1,2048,2304]{3,2,1,0:T(8,128)(2,1)}, f32[2048,2304]{1,0:T(8,128)}) fusion(f32[2048,2304]{1,0:T(8,128)} %fusion.172, bf16[2,896,2304]{2,1,0:T(8,128)(2,1)} %param.15, bf16[1,1,2048,896]{2,3,1,0:T(8,128)(2,1)} %copy-done), kind=kOutput, calls=%fused_computation.189 | convolution fusion | flops 8484028416 | bytes 54984704 | tf_op jit(solution)/vmap(jvp())/dot_general | solution.py:21
  121.4 30.9 %convert_multiply_fusion.2 = (bf16[1,1,2048,2304]{3,2,1,0:T(8,128)(2,1)}, bf16[1,1,2048,2304]{3,2,1,0:T(8,128)(2,1)}) fusion(f32[2048,2304]{1,0:T(8,128)} %fusion.172, f32[2048,2304]{1,0:T(8,128)} %get-tuple-element.270, bf16[2,2304,896]{2,1,0:T(8,128)(2,1)} %param.16, bf16[1,2048,896]{2,1,0:T(8,128)(2,1)} %param.17), kind=kOutput, calls=%fused_computation.172 | convolution fusion | flops 8531214336 | bytes 64421888 | tf_op jit(solution)/vmap(transpose(jvp()))/dot_general | solution.py:9
  152.3 13.1 %fusion.148 = bf16[2048,896]{0,1:T(8,128)(2,1)S(1)} fusion(bf16[1,1,2048,2304]{3,2,1,0:T(8,128)(2,1)} %get-tuple-element.545, bf16[2,896,2304]{2,1,0:T(8,128)(2,1)} %param.12), kind=kOutput, calls=%fused_computation.178 | convolution fusion | flops 8455716864 | bytes 17235968 | tf_op jit(solution)/vmap(transpose(jvp()))/dot_general | solution.py:20
  165.4 12.2 %fusion.170 = (f32[2048]{0:T(1024)S(1)}, bf16[2048,896]{0,1:T(8,128)(2,1)}) fusion(bf16[1,1,2048,896]{2,3,1,0:T(8,128)(2,1)S(1)} %copy-done.19, bf16[2048,896]{0,1:T(8,128)(2,1)S(1)} %fusion.148, bf16[2,896,2304]{2,1,0:T(8,128)(2,1)} %param.15, bf16[1,1,2048,2304]{3,2,1,0:T(8,128)(2,1)S(1)} %copy-done.5), kind=kOutput, calls=%fused_computation.217 | convolution fusion | flops 8464889856 | bytes 24584192 | tf_op jit(solution)/vmap(transpose(jvp()))/dot_general | solution.py:21
  177.7 9.1 fusion.187
  186.8 30.7 %convert_multiply_fusion = (bf16[1,1,2048,2304]{3,2,1,0:T(8,128)(2,1)}, bf16[1,1,2048,2304]{3,2,1,0:T(8,128)(2,1)}) fusion(f32[2048,2304]{1,0:T(8,128)} %fusion.182, f32[2048,2304]{1,0:T(8,128)} %get-tuple-element.264, bf16[2,2304,896]{2,1,0:T(8,128)(2,1)} %param.16, bf16[1,1,2048,896]{2,3,1,0:T(8,128)(2,1)} %fusion.187), kind=kOutput, calls=%fused_computation.170 | convolution fusion | flops 8531214336 | bytes 64421888 | tf_op jit(solution)/vmap(transpose(jvp()))/dot_general | solution.py:9
  217.5 93.1 %while.13 = (bf16[1,1,2048,896]{2,3,1,0:T(8,128)(2,1)}, bf16[1,1,2048,2304]{3,2,1,0:T(8,128)(2,1)}, f32[1,56,2304]{2,1,0:T(8,128)S(1)}, f32[1,56,2304]{2,1,0:T(8...) while((bf16[1,1,2048,896]{2,3,1,0:T(8,128)(2,1)}, ...), condition=%wide.windowed_dot_general_cond_rs.1.clone, body=%wide.windowed_dot_general_body_rs.1.clone.sunk | while | flops 2116538368 | bytes 97223328 | solution.py:20
  311.4 94.9 %while.12 = (bf16[1,1,2048,896]{2,3,1,0:T(8,128)(2,1)}, bf16[1,1,2048,2304]{3,2,1,0:T(8,128)(2,1)}, f32[1,56,2304]{2,1,0:T(8,128)S(1)}, f32[1,56,2304]{2,1,0:T(8...) while((bf16[1,1,2048,896]{2,3,1,0:T(8,128)(2,1)}, ...), condition=%wide.windowed_dot_general_cond_rs.clone, body=%wide.windowed_dot_general_body_rs.clone.sunk | while | flops 2116538368 | bytes 97223328 | solution.py:20
  407.1 94.8 %while.15 = (bf16[1,1,2048,896]{2,3,1,0:T(8,128)(2,1)}, bf16[1,1,2048,2304]{3,2,1,0:T(8,128)(2,1)}, f32[1,56,2304]{2,1,0:T(8,128)S(1)}, f32[1,56,2304]{2,1,0:T(8...) while((bf16[1,1,2048,896]{2,3,1,0:T(8,128)(2,1)}, ...), condition=%wide.windowed_dot_general_cond_rs.3.clone, body=%wide.windowed_dot_general_body_rs.3.clone.sunk | while | flops 2116538368 | bytes 97223328 | solution.py:21
  501.9 13.0 %copy.4 = bf16[1,1,2048,2304]{2,3,1,0:T(8,128)(2,1)} copy(bf16[1,1,2048,2304]{3,2,1,0:T(8,128)(2,1)} %get-tuple-element.263) | data formatting | bytes 18874368
  520.9 12.8 %copy.2 = bf16[1,1,2048,2304]{2,3,1,0:T(8,128)(2,1)} copy(bf16[1,1,2048,2304]{3,2,1,0:T(8,128)(2,1)} %get-tuple-element.269) | data formatting | bytes 18874368
  539.7 92.3 %while.14 = (bf16[1,1,2048,896]{2,3,1,0:T(8,128)(2,1)}, bf16[1,1,2048,2304]{3,2,1,0:T(8,128)(2,1)}, f32[1,56,2304]{2,1,0:T(8,128)S(1)}, f32[1,56,2304]{2,1,0:T(8...) while((bf16[1,1,2048,896]{2,3,1,0:T(8,128)(2,1)}, ...), condition=%wide.windowed_dot_general_cond_rs.2.clone, body=%wide.windowed_dot_general_body_rs.2.clone.sunk | while | flops 2116538368 | bytes 97223328 | solution.py:21
  632.9 86.5 %while.17 = (bf16[1,1,2048,2304]{2,3,1,0:T(8,128)(2,1)}, bf16[1,1,2048,896]{3,2,1,0:T(8,128)(2,1)}, f32[1,144,896]{2,1,0:T(8,128)S(1)}, f32[1,144,896]{2,1,0:T(8...) while((bf16[1,1,2048,2304]{2,3,1,0:T(8,128)(2,1)}, ...), condition=%wide.windowed_dot_general_cond_rs.5.clone, body=%wide.windowed_dot_general_body_rs.5.clone.sunk | while | flops 2119421952 | bytes 44794468 | solution.py:9
  720.1 105.2 %while.16 = (bf16[1,1,2048,2304]{2,3,1,0:T(8,128)(2,1)}, bf16[1,1,2048,896]{3,2,1,0:T(8,128)(2,1)}, f32[1,144,896]{2,1,0:T(8,128)S(1)}, f32[1,144,896]{2,1,0:T(8...) while((bf16[1,1,2048,2304]{2,3,1,0:T(8,128)(2,1)}, ...), condition=%wide.windowed_dot_general_cond_rs.4.clone, body=%wide.windowed_dot_general_body_rs.4.clone.sunk | while | flops 2119421952 | bytes 44794468 | solution.py:9
  845.0 30.4 %all-reduce.10 = f32[1]{0:T(128)} all-reduce(f32[1]{0:T(128)} %bitcast.39), channel_id=13, replica_groups=mesh['rep'=4,'dp'=16] {'dp'}, use_global_device_ids=true, to_apply=%region_3.4.clone | all-reduce | flops 1 | bytes 8 | tf_op jit(solution)/vmap()/reduce_sum | solution.py:54
  887.8 44.7 %all-gather.10.cloned.1.call-done = bf16[1,2,896,2304]{3,2,1,0:T(8,128)(2,1)} async-done(((bf16[1,2,56,2304]{3,2,1,0:T(8,128)(2,1)}), bf16[1,2,896,2304]{3,2,1,0:T(8,128)(2,1)}) %all-gather.10.cloned.1.call-update) | async-done | bytes 8257552 | tf_op jit(solution)/reshape | solution.py:58
  932.5 52.7 %all-gather.12.cloned.1.call-done = bf16[1,2,896,2304]{3,2,1,0:T(8,128)(2,1)} async-done(((bf16[1,2,56,2304]{3,2,1,0:T(8,128)(2,1)}), bf16[1,2,896,2304]{3,2,1,0:T(8,128)(2,1)}) %all-gather.12.cloned.1.call-update) | async-done | bytes 8257552 | tf_op jit(solution)/reshape | solution.py:58
  985.2 52.7 %all-gather.14.cloned.1.call-done = bf16[1,2,2304,896]{3,2,1,0:T(8,128)(2,1)} async-done(((bf16[1,2,144,896]{3,2,1,0:T(8,128)(2,1)}), bf16[1,2,2304,896]{3,2,1,0:T(8,128)(2,1)}) %all-gather.14.cloned.1.call-update) | async-done | bytes 8257552 | tf_op jit(solution)/reshape | solution.py:58
  1037.9 7.2 copy.63
  1052.3 7.3 copy.65
  (511 shorter events, 593.9 us)
Async XLA Ops:
  7.2 925.3 %all-gather.10.cloned.1.call-start = ((), (), s32[]{:S(2)}) async-start(), calls=%async_computation | async-start | bytes 8773632 | tf_op jit(solution)/reshape | solution.py:58
  217.5 12.9 %collective-permute-start.4 = (f32[1,56,2304]{2,1,0:T(8,128)S(1)}, f32[1,56,2304]{2,1,0:T(8,128)S(1)}, u32[]{:S(2)}, u32[]{:S(2)}) collective-permute-start(f32[1,56,2304]{2,1,0:T(8,128)S(1)} %broadcast_select_fusion.26), channel_id=9, source_target_pairs={{0,1},{1,2},{2,3},{3,4},{4,5},{5,6},{6,7},{7,8},{8,9},{9,10},{10,1... | collective-permute-start | bytes 1548296 | tf_op jit(solution)/vmap(transpose(jvp()))/dot_general | solution.py:20
  241.7 12.5 %collective-permute-start.4 = (f32[1,56,2304]{2,1,0:T(8,128)S(1)}, f32[1,56,2304]{2,1,0:T(8,128)S(1)}, u32[]{:S(2)}, u32[]{:S(2)}) collective-permute-start(f32[1,56,2304]{2,1,0:T(8,128)S(1)} %broadcast_select_fusion.26), channel_id=9, source_target_pairs={{0,1},{1,2},{2,3},{3,4},{4,5},{5,6},{6,7},{7,8},{8,9},{9,10},{10,1... | collective-permute-start | bytes 1548296 | tf_op jit(solution)/vmap(transpose(jvp()))/dot_general | solution.py:20
  241.8 12.4 %collective-permute-start.5 = (f32[1,56,2304]{2,1,0:T(8,128)S(1)}, f32[1,56,2304]{2,1,0:T(8,128)S(1)}, u32[]{:S(2)}, u32[]{:S(2)}) collective-permute-start(f32[1,56,2304]{2,1,0:T(8,128)S(1)} %broadcast_select_fusion.27), channel_id=8, source_target_pairs={{0,15},{1,0},{2,1},{3,2},{4,3},{5,4},{6,5},{7,6},{8,7},{9,8},{10,9... | collective-permute-start | bytes 1548296 | tf_op jit(solution)/vmap(transpose(jvp()))/dot_general | solution.py:20
  265.3 12.1 %collective-permute-start.4 = (f32[1,56,2304]{2,1,0:T(8,128)S(1)}, f32[1,56,2304]{2,1,0:T(8,128)S(1)}, u32[]{:S(2)}, u32[]{:S(2)}) collective-permute-start(f32[1,56,2304]{2,1,0:T(8,128)S(1)} %broadcast_select_fusion.26), channel_id=9, source_target_pairs={{0,1},{1,2},{2,3},{3,4},{4,5},{5,6},{6,7},{7,8},{8,9},{9,10},{10,1... | collective-permute-start | bytes 1548296 | tf_op jit(solution)/vmap(transpose(jvp()))/dot_general | solution.py:20
  288.5 12.1 %collective-permute-start.4 = (f32[1,56,2304]{2,1,0:T(8,128)S(1)}, f32[1,56,2304]{2,1,0:T(8,128)S(1)}, u32[]{:S(2)}, u32[]{:S(2)}) collective-permute-start(f32[1,56,2304]{2,1,0:T(8,128)S(1)} %broadcast_select_fusion.26), channel_id=9, source_target_pairs={{0,1},{1,2},{2,3},{3,4},{4,5},{5,6},{6,7},{7,8},{8,9},{9,10},{10,1... | collective-permute-start | bytes 1548296 | tf_op jit(solution)/vmap(transpose(jvp()))/dot_general | solution.py:20
  310.6 518.5 %collective-permute-start.25 = (f32[1,56,2304]{2,1,0:T(8,128)}, f32[1,56,2304]{2,1,0:T(8,128)}, u32[]{:S(2)}, u32[]{:S(2)}) collective-permute-start(f32[1,56,2304]{2,1,0:T(8,128)} %get-tuple-element.39), channel_id=12, source_target_pairs={{0,1},{1,2},{2,3},{3,4},{4,5},{5,6},{6,7},{7,8},{8,9},{9,10},{10,1... | collective-permute-start | bytes 1548296 | tf_op jit(solution)/vmap(transpose(jvp()))/dot_general | solution.py:20
  311.7 12.1 %collective-permute-start = (f32[1,56,2304]{2,1,0:T(8,128)S(1)}, f32[1,56,2304]{2,1,0:T(8,128)S(1)}, u32[]{:S(2)}, u32[]{:S(2)}) collective-permute-start(f32[1,56,2304]{2,1,0:T(8,128)S(1)} %broadcast_select_fusion.24), channel_id=3, source_target_pairs={{0,1},{1,2},{2,3},{3,4},{4,5},{5,6},{6,7},{7,8},{8,9},{9,10},{10,1... | collective-permute-start | bytes 1548296 | tf_op jit(solution)/vmap(transpose(jvp()))/dot_general | solution.py:20
  335.4 14.5 %collective-permute-start = (f32[1,56,2304]{2,1,0:T(8,128)S(1)}, f32[1,56,2304]{2,1,0:T(8,128)S(1)}, u32[]{:S(2)}, u32[]{:S(2)}) collective-permute-start(f32[1,56,2304]{2,1,0:T(8,128)S(1)} %broadcast_select_fusion.24), channel_id=3, source_target_pairs={{0,1},{1,2},{2,3},{3,4},{4,5},{5,6},{6,7},{7,8},{8,9},{9,10},{10,1... | collective-permute-start | bytes 1548296 | tf_op jit(solution)/vmap(transpose(jvp()))/dot_general | solution.py:20
  335.5 14.4 %collective-permute-start.1 = (f32[1,56,2304]{2,1,0:T(8,128)S(1)}, f32[1,56,2304]{2,1,0:T(8,128)S(1)}, u32[]{:S(2)}, u32[]{:S(2)}) collective-permute-start(f32[1,56,2304]{2,1,0:T(8,128)S(1)} %broadcast_select_fusion.25), channel_id=2, source_target_pairs={{0,15},{1,0},{2,1},{3,2},{4,3},{5,4},{6,5},{7,6},{8,7},{9,8},{10,9... | collective-permute-start | bytes 1548296 | tf_op jit(solution)/vmap(transpose(jvp()))/dot_general | solution.py:20
  361.0 12.0 %collective-permute-start = (f32[1,56,2304]{2,1,0:T(8,128)S(1)}, f32[1,56,2304]{2,1,0:T(8,128)S(1)}, u32[]{:S(2)}, u32[]{:S(2)}) collective-permute-start(f32[1,56,2304]{2,1,0:T(8,128)S(1)} %broadcast_select_fusion.24), channel_id=3, source_target_pairs={{0,1},{1,2},{2,3},{3,4},{4,5},{5,6},{6,7},{7,8},{8,9},{9,10},{10,1... | collective-permute-start | bytes 1548296 | tf_op jit(solution)/vmap(transpose(jvp()))/dot_general | solution.py:20
  384.2 12.0 %collective-permute-start = (f32[1,56,2304]{2,1,0:T(8,128)S(1)}, f32[1,56,2304]{2,1,0:T(8,128)S(1)}, u32[]{:S(2)}, u32[]{:S(2)}) collective-permute-start(f32[1,56,2304]{2,1,0:T(8,128)S(1)} %broadcast_select_fusion.24), channel_id=3, source_target_pairs={{0,1},{1,2},{2,3},{3,4},{4,5},{5,6},{6,7},{7,8},{8,9},{9,10},{10,1... | collective-permute-start | bytes 1548296 | tf_op jit(solution)/vmap(transpose(jvp()))/dot_general | solution.py:20
  406.3 424.0 %collective-permute-start.24 = (f32[1,56,2304]{2,1,0:T(8,128)}, f32[1,56,2304]{2,1,0:T(8,128)}, u32[]{:S(2)}, u32[]{:S(2)}) collective-permute-start(f32[1,56,2304]{2,1,0:T(8,128)} %get-tuple-element.37), channel_id=6, source_target_pairs={{0,1},{1,2},{2,3},{3,4},{4,5},{5,6},{6,7},{7,8},{8,9},{9,10},{10,1... | collective-permute-start | bytes 1548296 | tf_op jit(solution)/vmap(transpose(jvp()))/dot_general | solution.py:20
  407.1 12.0 %collective-permute-start.12 = (f32[1,56,2304]{2,1,0:T(8,128)S(1)}, f32[1,56,2304]{2,1,0:T(8,128)S(1)}, u32[]{:S(2)}, u32[]{:S(2)}) collective-permute-start(f32[1,56,2304]{2,1,0:T(8,128)S(1)} %broadcast_select_fusion.30), channel_id=22, source_target_pairs={{0,1},{1,2},{2,3},{3,4},{4,5},{5,6},{6,7},{7,8},{8,9},{9,10},{10,1... | collective-permute-start | bytes 1548296 | tf_op jit(solution)/vmap(transpose(jvp()))/dot_general | solution.py:21
  431.4 14.2 %collective-permute-start.12 = (f32[1,56,2304]{2,1,0:T(8,128)S(1)}, f32[1,56,2304]{2,1,0:T(8,128)S(1)}, u32[]{:S(2)}, u32[]{:S(2)}) collective-permute-start(f32[1,56,2304]{2,1,0:T(8,128)S(1)} %broadcast_select_fusion.30), channel_id=22, source_target_pairs={{0,1},{1,2},{2,3},{3,4},{4,5},{5,6},{6,7},{7,8},{8,9},{9,10},{10,1... | collective-permute-start | bytes 1548296 | tf_op jit(solution)/vmap(transpose(jvp()))/dot_general | solution.py:21
  431.5 14.1 %collective-permute-start.13 = (f32[1,56,2304]{2,1,0:T(8,128)S(1)}, f32[1,56,2304]{2,1,0:T(8,128)S(1)}, u32[]{:S(2)}, u32[]{:S(2)}) collective-permute-start(f32[1,56,2304]{2,1,0:T(8,128)S(1)} %broadcast_select_fusion.31), channel_id=21, source_target_pairs={{0,15},{1,0},{2,1},{3,2},{4,3},{5,4},{6,5},{7,6},{8,7},{9,8},{10,9... | collective-permute-start | bytes 1548296 | tf_op jit(solution)/vmap(transpose(jvp()))/dot_general | solution.py:21
  456.6 12.0 %collective-permute-start.12 = (f32[1,56,2304]{2,1,0:T(8,128)S(1)}, f32[1,56,2304]{2,1,0:T(8,128)S(1)}, u32[]{:S(2)}, u32[]{:S(2)}) collective-permute-start(f32[1,56,2304]{2,1,0:T(8,128)S(1)} %broadcast_select_fusion.30), channel_id=22, source_target_pairs={{0,1},{1,2},{2,3},{3,4},{4,5},{5,6},{6,7},{7,8},{8,9},{9,10},{10,1... | collective-permute-start | bytes 1548296 | tf_op jit(solution)/vmap(transpose(jvp()))/dot_general | solution.py:21
  479.8 12.0 %collective-permute-start.12 = (f32[1,56,2304]{2,1,0:T(8,128)S(1)}, f32[1,56,2304]{2,1,0:T(8,128)S(1)}, u32[]{:S(2)}, u32[]{:S(2)}) collective-permute-start(f32[1,56,2304]{2,1,0:T(8,128)S(1)} %broadcast_select_fusion.30), channel_id=22, source_target_pairs={{0,1},{1,2},{2,3},{3,4},{4,5},{5,6},{6,7},{7,8},{8,9},{9,10},{10,1... | collective-permute-start | bytes 1548296 | tf_op jit(solution)/vmap(transpose(jvp()))/dot_general | solution.py:21
  501.9 329.6 %collective-permute-start.27 = (f32[1,56,2304]{2,1,0:T(8,128)}, f32[1,56,2304]{2,1,0:T(8,128)}, u32[]{:S(2)}, u32[]{:S(2)}) collective-permute-start(f32[1,56,2304]{2,1,0:T(8,128)} %get-tuple-element.43), channel_id=25, source_target_pairs={{0,1},{1,2},{2,3},{3,4},{4,5},{5,6},{6,7},{7,8},{8,9},{9,10},{10,1... | collective-permute-start | bytes 1548296 | tf_op jit(solution)/vmap(transpose(jvp()))/dot_general | solution.py:21
  562.9 12.0 %collective-permute-start.8 = (f32[1,56,2304]{2,1,0:T(8,128)S(1)}, f32[1,56,2304]{2,1,0:T(8,128)}, u32[]{:S(2)}, u32[]{:S(2)}) collective-permute-start(f32[1,56,2304]{2,1,0:T(8,128)S(1)} %broadcast_select_fusion.28), channel_id=16, source_target_pairs={{0,1},{1,2},{2,3},{3,4},{4,5},{5,6},{6,7},{7,8},{8,9},{9,10},{10,1... | collective-permute-start | bytes 1548296 | tf_op jit(solution)/vmap(transpose(jvp()))/dot_general | solution.py:21
  609.1 12.0 %collective-permute-start.8 = (f32[1,56,2304]{2,1,0:T(8,128)S(1)}, f32[1,56,2304]{2,1,0:T(8,128)}, u32[]{:S(2)}, u32[]{:S(2)}) collective-permute-start(f32[1,56,2304]{2,1,0:T(8,128)S(1)} %broadcast_select_fusion.28), channel_id=16, source_target_pairs={{0,1},{1,2},{2,3},{3,4},{4,5},{5,6},{6,7},{7,8},{8,9},{9,10},{10,1... | collective-permute-start | bytes 1548296 | tf_op jit(solution)/vmap(transpose(jvp()))/dot_general | solution.py:21
  829.2 13.2 %collective-permute-start.28 = (f32[1,144,896]{2,1,0:T(8,128)}, f32[1,144,896]{2,1,0:T(8,128)}, u32[]{:S(2)}, u32[]{:S(2)}) collective-permute-start(f32[1,144,896]{2,1,0:T(8,128)} %get-tuple-element.45), channel_id=32, source_target_pairs={{0,1},{1,2},{2,3},{3,4},{4,5},{5,6},{6,7},{7,8},{8,9},{9,10},{10,1... | collective-permute-start | bytes 1548296 | tf_op jit(solution)/vmap(transpose(jvp()))/dot_general | solution.py:9
  880.1 105.1 %all-gather.12.cloned.1.call-start = ((), (), s32[]{:S(2)}) async-start(), calls=%async_computation.1 | async-start | bytes 8773632 | tf_op jit(solution)/reshape | solution.py:58
  883.9 153.9 %all-gather.14.cloned.1.call-start = ((), (), s32[]{:S(2)}) async-start(), calls=%async_computation.2 | async-start | bytes 8773632 | tf_op jit(solution)/reshape | solution.py:58
  (129 other events, 1478.7 us)
Sparse Core Ops, SparseCore 0:
  880.2 52.2 all-gather.9
  934.7 50.4 all-gather.11
  987.4 50.4 all-gather.13
where the time goes:
time: 1080 us; the launch traced here: 1070 us
  matrix products  348 us (32%)
  waiting for transfers between devices  250 us (23%)
  starting transfers between devices  174 us (16%)
  other arithmetic  103 us (10%)
  local copies, waits for them, and re-layouts  94 us (9%)
  loops' own time  49.1 us (5%)
  blocking collectives  30.4 us (3%)
  between operations  17.8 us (2%)
    reshape x3, waiting for transfers between devices, step(): t.reshape(-1, *t.shape[2:])  150 us
    dot_general x19, matrix products, matmul(): jnp.dot(a, w, preferred_element_type=jnp.float32).astype(jnp.bfloat16)  136 us
    dot_general x19, matrix products, layer(): up = jnp.dot(a, w['w_up'], preferred_element_type=jnp.float32)  113 us
    dot_general x19, matrix products, layer(): gate = jnp.dot(a, w['w_gate'], preferred_element_type=jnp.float32)  99.6 us
    unnamed x41, local copies, waits for them, and re-layouts  78.6 us
    dot_general x34, starting transfers between devices, layer(): gate = jnp.dot(a, w['w_gate'], preferred_element_type=jnp.float32)  63.2 us
    dot_general x34, starting transfers between devices, layer(): up = jnp.dot(a, w['w_up'], preferred_element_type=jnp.float32)  60.9 us
    dot_general x34, starting transfers between devices, matmul(): jnp.dot(a, w, preferred_element_type=jnp.float32).astype(jnp.bfloat16)  49.9 us
  transfers between devices with their start and end apart: 105, of which 50 were waited for; matrix products, arithmetic and copies ran while one was open for 28% of the time, Pallas kernels for 0%

commit v1 on v0

v1 whole, which is shorter than its diff:
```python
import jax
import jax.numpy as jnp
from jax import lax
from jax.sharding import PartitionSpec as P

NAMES = ("w_gate", "w_up", "w_down")


def matmul(a, w):
    return jnp.dot(a, w, preferred_element_type=jnp.float32).astype(jnp.bfloat16)


def normed(h):
    wide = h.astype(jnp.float32)
    scale = lax.rsqrt(jnp.mean(wide**2, -1, keepdims=True) + 1e-6)
    return (wide * scale).astype(jnp.bfloat16)


def layer(h, w_gate, w_up, w_down):
    a = normed(h)
    gate = jnp.dot(a, w_gate, preferred_element_type=jnp.float32)
    up = jnp.dot(a, w_up, preferred_element_type=jnp.float32)
    return h + matmul((jax.nn.silu(gate) * up).astype(jnp.bfloat16), w_down)


def adamw(w, m, v, g):
    m = 0.9 * m + 0.1 * g
    v = 0.95 * v + 0.05 * g * g
    step = m * lax.rsqrt(v + 1e-8) + 0.1 * w
    return (w - 0.02 * step).astype(jnp.bfloat16), m, v


def stack(weights, h):
    for one in weights:
        h = layer(h, *one)
    return h


def solution(mesh):
    members = mesh.shape["dp"]

    def body(x, dy, *arrays):
        weights, m, v = (arrays[i : i + 3] for i in (0, 3, 6))
        layers = weights[0].shape[0]
        _, back = jax.vjp(lambda w: stack(w, x[0]), [tuple(w[i] for w in weights) for i in range(layers)])
        by_weights = back(dy[0])[0]
        mine = {}
        for i in reversed(range(layers)):
            for k in (2, 0, 1):
                mine[k, i] = lax.psum_scatter(by_weights[i][k], "dp", scatter_dimension=0, tiled=True)
        gradients = [jnp.stack([mine[k, i] for i in range(layers)]).astype(jnp.float32) for k in range(3)]
        total = lax.psum(sum(jnp.sum(g * g) for g in gradients), "dp")
        factor = jnp.minimum(1.0, 0.5 * lax.rsqrt(total / sum(w.size for w in weights) + 1e-30))
        me = lax.axis_index("dp")
        new = []
        for w, m_, v_, g in zip(weights, m, v, gradients, strict=True):
            rows = w.shape[1] // members
            own = lax.dynamic_slice_in_dim(w, me * rows, rows, 1).astype(jnp.float32)
            new.append(adamw(own, m_, v_, g * factor))
        gathered = [lax.all_gather(one[0], "dp", axis=1, tiled=True) for one in new]
        return (*gathered, *(one[1] for one in new), *(one[2] for one in new))

    whole, rows = P(), P(None, "dp")
    tokens = P(("rep", "dp"))
    return jax.shard_map(
        body,
        mesh=mesh,
        in_specs=(tokens, tokens, *[whole] * 3, *[rows] * 6),
        out_specs=(*[P("rep")] * 3, *[P("rep", "dp")] * 6),
        check_vma=False,
    )
```

time: 1080 us -> 781 us (0.72)
  starting transfers between devices: 174 us -> 0.58 us
  waiting for transfers between devices: 250 us -> 406 us
  matrix products: 348 us -> 263 us
  other arithmetic: 103 us -> 21.8 us
  local copies, waits for them, and re-layouts: 94 us -> 35.8 us
  loops' own time: 49.1 us -> 0 us
    reduce_scatter x0 -> x6, waiting for transfers between devices: none -> 254 us  [body(): lax.psum_scatter(by_weights[i][k], 'dp', scatter_dimension=0, tiled=True)]
    dot_general x102 -> x0, starting transfers between devices: 174 us -> none  [the longest x34 63.2 us: layer(): gate = jnp.dot(a, w['w_gate'], preferred_element_type=jnp.float32)]
    all_gather x0 -> x3, waiting for transfers between devices: none -> 152 us  [body(): gathered = [lax.all_gather(one[0], 'dp', axis=1, tiled=True) for one in new]]
    reshape x3 -> x0, waiting for transfers between devices: 150 us -> none  [step(): t.reshape(-1, *t.shape[2:])]
    dot_general x102 -> x0, waiting for transfers between devices: 99.3 us -> none  [the longest x34 34 us: matmul(): jnp.dot(a, w, preferred_element_type=jnp.float32).astype(jnp.bfloat16)]
    dot_general x96 -> x0, other arithmetic: 65.4 us -> none  [the longest x16 23.4 us: matmul(): jnp.dot(a, w, preferred_element_type=jnp.float32).astype(jnp.bfloat16)]
    dot_general x19 -> x5, matrix products: 136 us -> 78.3 us  [matmul(): jnp.dot(a, w, preferred_element_type=jnp.float32).astype(jnp.bfloat16)]
    another operation x6 -> x0, loops' own time: 49.1 us -> none  [the longest x2 16.6 us: matmul(): jnp.dot(a, w, preferred_element_type=jnp.float32).astype(jnp.bfloat16)]
  transfers between devices with their start and end apart: 105 -> 9, of which waited for: 50 -> 8; matrix products, arithmetic and copies ran while one was open for 28% -> 15% of each run, Pallas kernels for 0% -> 0%
where the time goes in v1:
time: 781 us; the launch traced here: 772 us
  waiting for transfers between devices  406 us (52%)
  matrix products  263 us (34%)
  local copies, waits for them, and re-layouts  35.8 us (5%)
  blocking collectives  27.2 us (3%)
  other arithmetic  21.8 us (3%)
  between operations  17.1 us (2%)
    reduce_scatter x6, waiting for transfers between devices, body(): lax.psum_scatter(by_weights[i][k], 'dp', scatter_dimension=0, tiled=True)  254 us
    all_gather x3, waiting for transfers between devices, body(): gathered = [lax.all_gather(one[0], 'dp', axis=1, tiled=True) for one in new]  152 us
    dot_general x5, matrix products, layer(): gate = jnp.dot(a, w_gate, preferred_element_type=jnp.float32)  95.6 us
    dot_general x5, matrix products, layer(): up = jnp.dot(a, w_up, preferred_element_type=jnp.float32)  89.6 us
    dot_general x5, matrix products, matmul(): jnp.dot(a, w, preferred_element_type=jnp.float32).astype(jnp.bfloat16)  78.3 us
    unnamed x29, local copies, waits for them, and re-layouts  35.8 us
    psum x1, blocking collectives, body(): total = lax.psum(sum((jnp.sum(g * g) for g in gradients)), 'dp')  27.2 us
  transfers between devices with their start and end apart: 9, of which 8 were waited for; matrix products, arithmetic and copies ran while one was open for 15% of the time, Pallas kernels for 0%

profile of v1, /device:TPU:21, one launch (start us, length us, event | category | flops | bytes accessed | tf_op | source)
XLA Modules:
  0.0 772.1 jit_solution(3683857180144402832)
XLA Ops:
  22.2 15.2 %convolution_convert_fusion.1 = bf16[2048,2304]{1,0:T(8,128)(2,1)} fusion(bf16[2,2304,896]{2,1,0:T(8,128)(2,1)} %param.15, bf16[1,2048,896]{2,1,0:T(8,128)(2,1)} %param.12), kind=kOutput, calls=%fused_computation.27 | convolution fusion | flops 8460435456 | bytes 17235968 | tf_op jit(solution)/shard_map/transpose(jvp())/dot_general | solution.py:10
  37.4 15.5 %fusion.41 = f32[2048,2304]{1,0:T(8,128)} fusion(bf16[2,896,2304]{2,1,0:T(8,128)(2,1)} %param.13, bf16[1,2048,896]{2,1,0:T(8,128)(2,1)S(1)} %copy-done.2, f32[2048]{0:T(1024)S(1)} %add_rsqrt_fusion), kind=kOutput, calls=%fused_computation.60 | convolution fusion | flops 8461221888 | bytes 26681344 | tf_op jit(solution)/shard_map/jvp()/dot_general | solution.py:21
  52.9 21.2 %multiply_convert_fusion.1 = (bf16[2048,2304]{1,0:T(8,128)(2,1)}, f32[2048,2304]{1,0:T(8,128)}) fusion(f32[2048,2304]{1,0:T(8,128)} %fusion.41, bf16[2,896,2304]{2,1,0:T(8,128)(2,1)} %param.14, bf16[1,2048,896]{2,1,0:T(8,128)(2,1)} %param.11, f32[2048]{0:T(1024)S(1)} %add_rsqrt_fusion), kind=kOutput, calls=%fused_computation.17 | convolution fusion | flops 8489533440 | bytes 54992896 | tf_op jit(solution)/shard_map/jvp()/dot_general | solution.py:22
  74.1 13.8 %fusion.19 = (f32[2048]{0:T(1024)S(1)}, bf16[2048,896]{0,1:T(8,128)(2,1)S(1)}) fusion(bf16[2048,2304]{1,0:T(8,128)(2,1)} %get-tuple-element.18, bf16[2,2304,896]{2,1,0:T(8,128)(2,1)} %param.15, bf16[1,2048,896]{1,2,0:T(8,128)(2,1)} %copy.20), kind=kOutput, calls=%fused_computation.37 | convolution fusion | flops 8464889856 | bytes 20914176 | tf_op jit(solution)/shard_map/jvp()/dot_general | solution.py:10
  88.0 16.3 %fusion.28 = f32[2048,2304]{1,0:T(8,128)} fusion(bf16[2,896,2304]{2,1,0:T(8,128)(2,1)} %param.14, bf16[2048,896]{0,1:T(8,128)(2,1)S(1)} %get-tuple-element.21, f32[2048]{0:T(1024)S(1)} %fusion.90), kind=kOutput, calls=%fused_computation.47 | convolution fusion | flops 8461221888 | bytes 26681344 | tf_op jit(solution)/shard_map/jvp()/dot_general | solution.py:22
  104.3 26.2 %fusion.2 = (bf16[2048,2304]{1,0:T(8,128)(2,1)}, f32[2048,2304]{1,0:T(8,128)}) fusion(f32[2048,2304]{1,0:T(8,128)} %fusion.28, bf16[2048,2304]{1,0:T(8,128)(2,1)} %convolution_convert_fusion.1, bf16[2,896,2304]{2,1,0:T(8,128)(2,1)} %param.13, bf16[2048,896]{0,1:T(8,128)(2,1)S(1)} %get-tuple-element.21, f32[2048]{0:T(1024)S(1)} %fusion.90), kind=kOutput, calls=%fused_computation.8 | convolution fusion | flops 8517844992 | bytes 64430080 | tf_op jit(solution)/shard_map/jvp()/dot_general | solution.py:21
  130.6 16.8 %fusion.12 = bf16[2048,896]{0,1:T(8,128)(2,1)} fusion(bf16[2048,2304]{1,0:T(8,128)(2,1)} %convolution_convert_fusion.1, bf16[2,896,2304]{2,1,0:T(8,128)(2,1)} %param.14, f32[2048,2304]{1,0:T(8,128)} %get-tuple-element.23), kind=kOutput, calls=%fused_computation.21 | convolution fusion | flops 8484028416 | bytes 36110336 | tf_op jit(solution)/shard_map/transpose(jvp())/dot_general | solution.py:22
  147.4 15.3 %fusion.21 = (f32[2048]{0:T(1024)S(1)}, bf16[2048,896]{0,1:T(8,128)(2,1)S(1)}) fusion(bf16[2048,896]{0,1:T(8,128)(2,1)} %copy-done.3, bf16[2048,896]{0,1:T(8,128)(2,1)} %fusion.12, bf16[2048,2304]{1,0:T(8,128)(2,1)} %get-tuple-element.22, bf16[2,896,2304]{2,1,0:T(8,128)(2,1)} %param.13), kind=kOutput, calls=%fused_computation.39 | convolution fusion | flops 8464889856 | bytes 24584192 | tf_op jit(solution)/shard_map/transpose(jvp())/dot_general | solution.py:21
  167.7 14.3 %convolution_convert_fusion.2 = bf16[2304,896]{1,0:T(8,128)(2,1)} fusion(bf16[2048,2304]{1,0:T(8,128)(2,1)} %get-tuple-element.18, bf16[2048,896]{0,1:T(8,128)(2,1)S(1)} %fusion.47), kind=kOutput, calls=%fused_computation.45 | convolution fusion | flops 8457781248 | bytes 17235968 | tf_op jit(solution)/shard_map/transpose(jvp())/dot_general | solution.py:10
  182.1 19.6 %fusion.22 = bf16[2304,896]{1,0:T(8,128)(2,1)} fusion(f32[2048,2304]{1,0:T(8,128)} %fusion.28, bf16[1,2048,896]{2,1,0:T(8,128)(2,1)} %param.12, f32[2048,2304]{1,0:T(8,128)} %get-tuple-element.23), kind=kOutput, calls=%fused_computation.41 | convolution fusion | flops 8486092800 | bytes 45547520 | tf_op jit(solution)/shard_map/transpose(jvp())/dot_general | solution.py:10
  201.8 15.4 %convolution_convert_fusion = bf16[2048,2304]{1,0:T(8,128)(2,1)} fusion(bf16[2048,896]{0,1:T(8,128)(2,1)} %copy-done.5, bf16[2,2304,896]{2,1,0:T(8,128)(2,1)} %param.15), kind=kOutput, calls=%fused_computation.26 | convolution fusion | flops 8460435456 | bytes 17235968 | tf_op jit(solution)/shard_map/transpose(jvp())/dot_general | solution.py:10
  217.3 17.0 %fusion.27 = bf16[896,2304]{1,0:T(8,128)(2,1)} fusion(bf16[2048,2304]{1,0:T(8,128)(2,1)} %convolution_convert_fusion, bf16[1,2048,896]{1,2,0:T(8,128)(2,1)S(1)} %copy-done, f32[2048]{0:T(1024)S(1)} %copy-done.11, f32[2048,2304]{1,0:T(8,128)} %fusion.41), kind=kOutput, calls=%fused_computation.44 | convolution fusion | flops 8491597824 | bytes 36118528 | tf_op jit(solution)/shard_map/transpose(jvp())/dot_general | solution.py:22
  234.5 18.2 %fusion.23 = bf16[896,2304]{1,0:T(8,128)(2,1)} fusion(bf16[2048,2304]{1,0:T(8,128)(2,1)} %convolution_convert_fusion.1, bf16[2048,896]{0,1:T(8,128)(2,1)} %copy-done.3, f32[2048]{0:T(1024)S(1)} %fusion.90, f32[2048,2304]{1,0:T(8,128)} %get-tuple-element.23), kind=kOutput, calls=%fused_computation.42 | convolution fusion | flops 8491597824 | bytes 36118528 | tf_op jit(solution)/shard_map/transpose(jvp())/dot_general | solution.py:22
  252.8 23.6 %fusion.24 = bf16[896,2304]{1,0:T(8,128)(2,1)} fusion(f32[2048,2304]{1,0:T(8,128)} %fusion.41, f32[2048,2304]{1,0:T(8,128)} %get-tuple-element.19, bf16[2048,2304]{1,0:T(8,128)(2,1)} %convolution_convert_fusion, bf16[1,2048,896]{1,2,0:T(8,128)(2,1)} %copy.20, f32[2048]{0:T(1024)S(1)} %copy-done.11), kind=kOutput, calls=%fused_computation.43 | convolution fusion | flops 8515190784 | bytes 54992896 | tf_op jit(solution)/shard_map/transpose(jvp())/dot_general | solution.py:21
  276.5 14.9 %convolution_convert_fusion.3 = bf16[896,2304]{1,0:T(8,128)(2,1)} fusion(bf16[2048,2304]{1,0:T(8,128)(2,1)} %get-tuple-element.22, bf16[2048,896]{0,1:T(8,128)(2,1)} %copy-done.3, f32[2048]{0:T(1024)S(1)} %fusion.90), kind=kOutput, calls=%fused_computation.46 | convolution fusion | flops 8461221888 | bytes 17244160 | tf_op jit(solution)/shard_map/transpose(jvp())/dot_general | solution.py:21
  291.5 13.1 %reduce-scatter.17.cloned.1.call-done = bf16[144,896]{1,0:T(8,128)(2,1)} async-done(((bf16[2304,896]{1,0:T(8,128)(2,1)}), bf16[144,896]{1,0:T(8,128)(2,1)}) %reduce-scatter.17.cloned.1.call-update) | async-done | bytes 258064 | tf_op jit(solution)/shard_map/reduce_scatter | solution.py:50
  306.5 59.0 %reduce-scatter.11.cloned.1.call-done = bf16[56,2304]{1,0:T(8,128)(2,1)} async-done(((bf16[896,2304]{1,0:T(8,128)(2,1)}), bf16[56,2304]{1,0:T(8,128)(2,1)}) %reduce-scatter.11.cloned.1.call-update) | async-done | bytes 258064 | tf_op jit(solution)/shard_map/reduce_scatter | solution.py:50
  365.5 61.3 %reduce-scatter.13.cloned.1.call-done = bf16[56,2304]{1,0:T(8,128)(2,1)} async-done(((bf16[896,2304]{1,0:T(8,128)(2,1)}), bf16[56,2304]{1,0:T(8,128)(2,1)}) %reduce-scatter.13.cloned.1.call-update) | async-done | bytes 258064 | tf_op jit(solution)/shard_map/reduce_scatter | solution.py:50
  428.8 59.4 %reduce-scatter.7.cloned.1.call-done = bf16[56,2304]{1,0:T(8,128)(2,1)} async-done(((bf16[896,2304]{1,0:T(8,128)(2,1)}), bf16[56,2304]{1,0:T(8,128)(2,1)}) %reduce-scatter.7.cloned.1.call-update) | async-done | bytes 258064 | tf_op jit(solution)/shard_map/reduce_scatter | solution.py:50
  488.2 61.3 %reduce-scatter.9.cloned.1.call-done = bf16[56,2304]{1,0:T(8,128)(2,1)} async-done(((bf16[896,2304]{1,0:T(8,128)(2,1)}), bf16[56,2304]{1,0:T(8,128)(2,1)}) %reduce-scatter.9.cloned.1.call-update) | async-done | bytes 258064 | tf_op jit(solution)/shard_map/reduce_scatter | solution.py:50
  553.4 27.2 %psum.7 = f32[]{:T(128)} all-reduce(f32[]{:T(128)S(6)} %add.104), channel_id=1, replica_groups=mesh['rep'=4,'dp'=16] {'dp'}, use_global_device_ids=true, to_apply=%region_12.13 | all-reduce | flops 1 | bytes 8 | tf_op jit(solution)/shard_map/psum | solution.py:52
  591.8 46.2 %all-gather.8.cloned.1.call-done = bf16[2,2304,896]{2,1,0:T(8,128)(2,1)} async-done(((bf16[2,144,896]{2,1,0:T(8,128)(2,1)}), bf16[2,2304,896]{2,1,0:T(8,128)(2,1)}) %all-gather.8.cloned.1.call-update) | async-done | bytes 8257552 | tf_op jit(solution)/shard_map/all_gather | solution.py:60
  638.0 52.7 %all-gather.6.cloned.1.call-done = bf16[2,896,2304]{2,1,0:T(8,128)(2,1)} async-done(((bf16[2,56,2304]{2,1,0:T(8,128)(2,1)}), bf16[2,896,2304]{2,1,0:T(8,128)(2,1)}) %all-gather.6.cloned.1.call-update) | async-done | bytes 8257552 | tf_op jit(solution)/shard_map/all_gather | solution.py:60
  690.6 52.7 %all-gather.4.cloned.1.call-done = bf16[2,896,2304]{2,1,0:T(8,128)(2,1)} async-done(((bf16[2,56,2304]{2,1,0:T(8,128)(2,1)}), bf16[2,896,2304]{2,1,0:T(8,128)(2,1)}) %all-gather.4.cloned.1.call-update) | async-done | bytes 8257552 | tf_op jit(solution)/shard_map/all_gather | solution.py:60
  (59 shorter events, 58.6 us)
Async XLA Ops:
  7.2 284.3 %reduce-scatter.15.cloned.1.call-start = ((), (), s32[]{:S(2)}) async-start(), calls=%async_computation.10 | async-start | bytes 4386816 | tf_op jit(solution)/shard_map/reduce_scatter | solution.py:50
  16.1 36.8 %copy-start.10 = (f32[2048]{0:T(1024)}, f32[2048]{0:T(1024)S(1)}, u32[]{:S(2)}) copy-start(f32[2048]{0:T(1024)S(1)} %add_rsqrt_fusion) | copy-start | bytes 24580
  22.2 15.2 %copy-start.2 = (bf16[1,2048,896]{2,1,0:T(8,128)(2,1)S(1)}, bf16[1,2048,896]{2,1,0:T(8,128)(2,1)}, u32[]{:S(2)}) copy-start(bf16[1,2048,896]{2,1,0:T(8,128)(2,1)} %param.11) | copy-start | bytes 11010052
  87.9 16.4 %copy-start.3 = (bf16[2048,896]{0,1:T(8,128)(2,1)}, bf16[2048,896]{0,1:T(8,128)(2,1)S(1)}, u32[]{:S(2)}) copy-start(bf16[2048,896]{0,1:T(8,128)(2,1)S(1)} %get-tuple-element.21) | copy-start | bytes 11010052
  147.4 15.4 %copy-start.1 = (bf16[1,2048,896]{1,2,0:T(8,128)(2,1)S(1)}, bf16[1,2048,896]{1,2,0:T(8,128)(2,1)}, u32[]{:S(2)}) copy-start(bf16[1,2048,896]{1,2,0:T(8,128)(2,1)} %copy.21) | copy-start | bytes 11010052
  147.4 15.4 %copy-start.4 = (bf16[2048,896]{0,1:T(8,128)(2,1)S(1)}, bf16[2048,896]{0,1:T(8,128)(2,1)}, u32[]{:S(2)}) copy-start(bf16[2048,896]{0,1:T(8,128)(2,1)} %copy-done.3) | copy-start | bytes 11010052
  165.8 1.8 copy-start.5
  182.0 122.6 %reduce-scatter.17.cloned.1.call-start = ((), (), s32[]{:S(2)}) async-start(), calls=%async_computation.11 | async-start | bytes 4386816 | tf_op jit(solution)/shard_map/reduce_scatter | solution.py:50
  201.7 15.5 %copy-start.11 = (f32[2048]{0:T(1024)S(1)}, f32[2048]{0:T(1024)}, u32[]{:S(2)}) copy-start(f32[2048]{0:T(1024)} %copy-done.10) | copy-start | bytes 24580
  201.8 163.7 %reduce-scatter.11.cloned.1.call-start = ((), (), s32[]{:S(2)}) async-start(), calls=%async_computation.8 | async-start | bytes 4386816 | tf_op jit(solution)/shard_map/reduce_scatter | solution.py:50
  201.8 15.5 %copy-start = (bf16[1,2048,896]{1,2,0:T(8,128)(2,1)S(1)}, bf16[1,2048,896]{1,2,0:T(8,128)(2,1)}, u32[]{:S(2)}) copy-start(bf16[1,2048,896]{1,2,0:T(8,128)(2,1)} %copy.20) | copy-start | bytes 11010052
  234.4 192.4 %reduce-scatter.13.cloned.1.call-start = ((), (), s32[]{:S(2)}) async-start(), calls=%async_computation.9 | async-start | bytes 4386816 | tf_op jit(solution)/shard_map/reduce_scatter | solution.py:50
  252.7 235.4 %reduce-scatter.7.cloned.1.call-start = ((), (), s32[]{:S(2)}) async-start(), calls=%async_computation.6 | async-start | bytes 4386816 | tf_op jit(solution)/shard_map/reduce_scatter | solution.py:50
  276.4 304.9 %copy-start.8 = (f32[2,144,896]{2,1,0:T(8,128)S(1)}, f32[2,144,896]{2,1,0:T(8,128)}, u32[]{:S(2)}) copy-start(f32[2,144,896]{2,1,0:T(8,128)} %param.21) | copy-start | bytes 3096580
  276.4 304.9 %copy-start.9 = (f32[2,144,896]{2,1,0:T(8,128)S(1)}, f32[2,144,896]{2,1,0:T(8,128)}, u32[]{:S(2)}) copy-start(f32[2,144,896]{2,1,0:T(8,128)} %param.18) | copy-start | bytes 3096580
  276.4 273.1 %reduce-scatter.9.cloned.1.call-start = ((), (), s32[]{:S(2)}) async-start(), calls=%async_computation.7 | async-start | bytes 4386816 | tf_op jit(solution)/shard_map/reduce_scatter | solution.py:50
  291.4 346.5 %all-gather.8.cloned.1.call-start = ((), (), s32[]{:S(2)}) async-start(), calls=%async_computation.14 | async-start | bytes 8773632 | tf_op jit(solution)/shard_map/all_gather | solution.py:60
  488.2 100.1 %copy-start.6 = (bf16[56,2304]{1,0:T(8,128)(2,1)S(1)}, bf16[56,2304]{1,0:T(8,128)(2,1)}, u32[]{:S(2)}) copy-start(bf16[56,2304]{1,0:T(8,128)(2,1)} %reduce-scatter.7.cloned.1.call-done) | copy-start | bytes 774148
  549.5 38.8 %copy-start.7 = (bf16[56,2304]{1,0:T(8,128)(2,1)S(1)}, bf16[56,2304]{1,0:T(8,128)(2,1)}, u32[]{:S(2)}) copy-start(bf16[56,2304]{1,0:T(8,128)(2,1)} %reduce-scatter.9.cloned.1.call-done) | copy-start | bytes 774148
  584.4 106.2 %all-gather.6.cloned.1.call-start = ((), (), s32[]{:S(2)}) async-start(), calls=%async_computation.13 | async-start | bytes 8773632 | tf_op jit(solution)/shard_map/all_gather | solution.py:60
  588.2 155.1 %all-gather.4.cloned.1.call-start = ((), (), s32[]{:S(2)}) async-start(), calls=%async_computation.12 | async-start | bytes 8773632 | tf_op jit(solution)/shard_map/all_gather | solution.py:60
Sparse Core Ops, SparseCore 0:
  182.2 61.5 reduce-scatter.14
  246.1 58.4 reduce-scatter.16
  307.0 58.5 reduce-scatter.10
  368.3 58.5 reduce-scatter.12
  429.6 58.5 reduce-scatter.6
  490.9 58.5 reduce-scatter.8
  584.5 53.3 all-gather.7
  640.2 50.4 all-gather.5
  692.9 50.4 all-gather.3
